TPU v7x, 256 devices: a whole 4x4x8 slice. The times are simulated.
256 devices in a mesh: rows: 32 (over z, y), cols: 8 (over x, core).
Axes of the slice: x: 4, y: 4, z: 8, core: 2. Of those that a mesh axis runs over, the one named last changes fastest.
Arguments:
- weight_up: bfloat16 [12288, 49152], P('rows', 'cols'), may hold values from -0.109375 to 0.109375
- low_up: bfloat16 [12288, 64], P('rows'), may hold values from -0.0546875 to 0.0546875
- high_up: bfloat16 [64, 49152], P(None, 'cols'), may hold values from -0.75 to 0.75
- norm_train: float32 [12288], P(('rows', 'cols')), may hold values from 0.25 to 1.75
- norm_step: float32 [12288], P(('rows', 'cols')), may hold values from -0.3 to 0.3
Outputs:
- serve_up: bfloat16 [12288, 49152], P(None, ('cols', 'rows'))
- scale_up: float32 [49152], P(('cols', 'rows'))
- serve_norm: bfloat16 [12288], replicated
All inputs are finite; a program needn't handle non-finite values.
Results may differ from a plain program's by a relative error of at most 0.0004.
Values may be sent and summed in bfloat16 or wider, within the bound.
A program may use at most 64 MiB of HBM per device.

v0:
```python
import jax
import jax.numpy as jnp
from jax import lax
from jax.sharding import Mesh
from jax.sharding import PartitionSpec as P

ROWS = ("rows_0", "rows_1")
ROWS_COLS = ("rows_0", "rows_1", "cols_0", "cols_1")
COLS = ("cols_0", "cols_1")
COLS_ROWS = ("cols_0", "cols_1", "rows_0", "rows_1")
mix_rate = 0.5


def copy_for_each(x, axis):
    copies = jnp.broadcast_to(x, (lax.axis_size(axis), *x.shape))
    return lax.all_to_all(copies, axis, split_axis=0, concat_axis=0, tiled=True)


def of_everyone(x, axis):
    return copy_for_each(x, axis).sum(axis=0)


def joined_along(pieces, dim):
    shape = list(pieces.shape[1:])
    shape[dim] *= pieces.shape[0]
    return jnp.moveaxis(pieces, 0, dim).reshape(shape)


def stacked_from(x, axes, sequence):
    pieces = x[None]
    for k in sequence:
        pieces = lax.all_gather(pieces, axes[k], axis=0, tiled=True)
    block = [lax.axis_size(axes[k]) for k in reversed(sequence)]
    pieces = pieces.reshape(*block, *x.shape)
    turned = sorted(range(len(sequence)), key=lambda place: sequence[len(sequence) - 1 - place])
    return pieces.transpose(*turned, *range(len(sequence), pieces.ndim)).reshape(-1, *x.shape)


def gathered_by_axis(x, axes, sequence, dim):
    return joined_along(stacked_from(x, axes, sequence), dim)


def per_device(weight_up, low_up, high_up, norm_train, norm_step):
    fresh_up = weight_up.astype(jnp.float32) + mix_rate * jnp.dot(
        low_up, high_up, preferred_element_type=jnp.float32
    )
    total_up = of_everyone(jnp.sum(fresh_up * fresh_up, axis=0), ROWS)
    scale_up = jnp.sqrt(total_up)
    narrow_up = (fresh_up / scale_up).astype(jnp.bfloat16)
    serve_up = lax.all_to_all(narrow_up, ROWS, split_axis=1, concat_axis=0, tiled=True)
    place = lax.axis_index(ROWS)
    scale_up = lax.dynamic_slice_in_dim(scale_up, place * serve_up.shape[1], serve_up.shape[1])
    serve_norm = gathered_by_axis(
        (norm_train + norm_step).astype(jnp.bfloat16), ROWS_COLS, (1, 0, 2, 3), 0
    )
    return (serve_up, scale_up, serve_norm)


def solution(mesh):
    split = Mesh(mesh.devices.reshape(8, 4, 4, 2), ("rows_0", "rows_1", "cols_0", "cols_1"))
    in_specs = (P(ROWS, COLS), P(ROWS, None), P(None, COLS), P(ROWS_COLS), P(ROWS_COLS))
    out_specs = (P(None, COLS_ROWS), P(COLS_ROWS), P())
    return jax.shard_map(
        per_device, mesh=split, in_specs=in_specs, out_specs=out_specs, check_vma=False
    )
```

profile of v0, /device:TPU:1, one launch (start us, length us, event | category | flops | bytes accessed | tf_op | source)
XLA Modules:
  0.0 198.1 jit_solution(16278709822635123350)
XLA Ops:
  0.6 0.0 copy-start
  0.6 1.1 copy-done
  1.8 8.0 %multiply_reduce_fusion = (f32[6144]{0:T(1024)S(1)}, f32[384,6144]{1,0:T(8,128)}) fusion(bf16[384,64]{0,1:T(8,128)(2,1)} %param.6, bf16[64,6144]{1,0:T(8,128)(2,1)S(1)} %copy-done, bf16[384,6144]{1,0:T(8,128)(2,1)} %param.5), kind=kOutput, calls=%fused_computation.1 | convolution fusion | flops 313780224 | bytes 15015936 | tf_op jit(solution)/shard_map/dot_general | solution.py:44
  9.8 0.4 broadcast_in_dim.7
  10.2 32.9 %all_to_all.25 = f32[32,1,6144]{2,1,0:T(1,128)S(1)} all-to-all(f32[32,1,6144]{2,1,0:T(1,128)S(1)} %broadcast_in_dim.7), channel_id=1, replica_groups=mesh['rows_0'=8,'rows_1'=4,'cols_0'=4,'cols_1'=2] {'rows_0','rows_1'}, dimensions={0} | all-to-all | bytes 1572864 | tf_op jit(solution)/shard_map/all_to_all | solution.py:16
  43.1 0.5 reduce_sum.19
  43.6 6.8 %divide_convert_fusion = bf16[384,6144]{1,0:T(8,128)(2,1)} fusion(f32[384,6144]{1,0:T(8,128)} %get-tuple-element.4, f32[6144]{0:T(1024)S(1)} %sqrt.7), kind=kLoop, calls=%fused_computation | loop fusion | flops 4718592 | bytes 14180352 | tf_op jit(solution)/shard_map/convert_element_type | solution.py:49
  50.4 0.0 copy-start.3
  50.4 0.0 copy-start.1
  50.4 0.0 copy-start.2
  50.4 6.7 %copy.20 = bf16[384,6144]{0,1:T(8,128)(2,1)} copy(bf16[384,6144]{1,0:T(8,128)(2,1)} %divide_convert_fusion) | data formatting | bytes 9437184 | tf_op jit(solution)/shard_map/convert_element_type | solution.py:49
  57.2 5.9 %all-to-all-start.1 = ((bf16[384,32,192]{0,2,1:T(8,128)(2,1)}), bf16[384,32,192]{0,2,1:T(8,128)(2,1)}, u32[]{:S(2)}, u32[]{:S(2)}) async-start(bf16[384,32,192]{0,2,1:T(8,128)(2,1)} %bitcast.11), calls=%async_computation.1 | async-start | bytes 9437184 | tf_op jit(solution)/shard_map/all_to_all | solution.py:50
  63.1 0.0 copy-done.3
  63.1 0.6 dynamic-slice
  64.3 0.0 copy-done.1
  64.3 0.0 copy-done.2
  64.4 0.2 dynamic-update-slice
  64.6 12.9 %all-reduce = bf16[192]{0:T(256)(128)(2,1)S(1)} all-reduce(bf16[192]{0:T(256)(128)(2,1)S(1)} %dynamic-update-slice), channel_id=2, replica_groups=mesh['rows_0'=8,'rows_1'=4,'cols_0'=4,'cols_1'=2] {'rows_1'}, use_global_device_ids=true, to_apply=%add | all-reduce | flops 192 | bytes 768
  77.6 0.1 reshape.24
  77.6 95.8 %all-gather.1 = bf16[8,4,48]{2,1,0:T(4,128)(2,1)S(1)} all-gather(bf16[1,4,48]{2,1,0:T(4,128)(2,1)S(1)} %reshape.24), channel_id=1, replica_groups=mesh['rows_0'=8,'rows_1'=4,'cols_0'=4,'cols_1'=2] {'rows_0'}, dimensions={0}, use_global_device_ids=true | all-gather | bytes 3456 | tf_op jit(solution)/shard_map/all_gather | solution.py:32
  173.4 9.6 %all_gather.14 = bf16[128,48]{1,0:T(8,128)(2,1)S(1)} all-gather(bf16[32,48]{1,0:T(8,128)(2,1)S(1)} %bitcast.14), channel_id=1, replica_groups=mesh['rows_0'=8,'rows_1'=4,'cols_0'=4,'cols_1'=2] {'cols_0'}, dimensions={0}, use_global_device_ids=true | all-gather | bytes 15360 | tf_op jit(solution)/shard_map/all_gather | solution.py:32
  183.0 8.3 %all_gather.15 = bf16[256,48]{1,0:T(8,128)(2,1)S(1)} all-gather(bf16[128,48]{1,0:T(8,128)(2,1)S(1)} %all_gather.14), channel_id=1, replica_groups=mesh['rows_0'=8,'rows_1'=4,'cols_0'=4,'cols_1'=2] {'cols_1'}, dimensions={0}, use_global_device_ids=true | all-gather | bytes 36864 | tf_op jit(solution)/shard_map/all_gather | solution.py:32
  191.3 0.1 copy.22
  191.4 0.7 reshape_reshape.3
  192.1 0.6 dynamic_slice.3
  192.8 0.0 all-to-all-done.1
  192.8 5.3 %copy.24 = bf16[32,24,8,384]{3,2,0,1:T(8,128)(2,1)} copy(bf16[32,24,8,384]{3,2,1,0:T(8,128)(2,1)} %bitcast.7) | data formatting | bytes 9437184 | tf_op jit(solution)/shard_map/all_to_all | solution.py:50
  (3 shorter events, 0.0 us)
Async XLA Ops:
  0.6 1.1 copy-start
  50.4 12.7 %copy-start.3 = (u32[256]{0:T(256)S(1)}, u32[256]{0:T(256)}, u32[]{:S(2)}) copy-start(u32[256]{0:T(256)} %constant.26) | copy-start | bytes 3076
  50.4 13.9 %copy-start.1 = (f32[48]{0:T(128)S(1)}, f32[48]{0:T(128)}, u32[]{:S(2)}) copy-start(f32[48]{0:T(128)} %param.8) | copy-start | bytes 580
  50.4 13.9 %copy-start.2 = (f32[48]{0:T(128)S(1)}, f32[48]{0:T(128)}, u32[]{:S(2)}) copy-start(f32[48]{0:T(128)} %param.9) | copy-start | bytes 580
  57.2 135.6 %all-to-all-start.1 = ((bf16[384,32,192]{0,2,1:T(8,128)(2,1)}), bf16[384,32,192]{0,2,1:T(8,128)(2,1)}, u32[]{:S(2)}, u32[]{:S(2)}) async-start(bf16[384,32,192]{0,2,1:T(8,128)(2,1)} %bitcast.11), calls=%async_computation.1 | async-start | bytes 9437184 | tf_op jit(solution)/shard_map/all_to_all | solution.py:50
where the time goes:
time: 199 us; the launch traced here: 198 us
  blocking collectives  160 us (80%)
  local copies, waits for them, and re-layouts  16 us (8%)
  matrix products  8.02 us (4%)
  other arithmetic  7.29 us (4%)
  starting transfers between devices  5.9 us (3%)
    all_gather x3, blocking collectives, stacked_from(): pieces = lax.all_gather(pieces, axes[k], axis=0, tiled=True)  114 us
    all_to_all x1, blocking collectives, copy_for_each(): return lax.all_to_all(copies, axis, split_axis=0, concat_axis=0, tiled=True)  32.9 us
    unnamed x1, blocking collectives  12.9 us
    dot_general x1, matrix products, per_device(): jnp.dot(low_up, high_up, preferred_element_type=jnp.float32)  8.02 us
    convert_element_type x1, other arithmetic, per_device(): narrow_up = (fresh_up / scale_up).astype(jnp.bfloat16)  6.83 us
    convert_element_type x1, local copies, waits for them, and re-layouts, per_device(): narrow_up = (fresh_up / scale_up).astype(jnp.bfloat16)  6.75 us
    all_to_all x1, starting transfers between devices, per_device(): lax.all_to_all(narrow_up, ROWS, split_axis=1, concat_axis=0, tiled=True)  5.9 us
    all_to_all x1, local copies, waits for them, and re-layouts, per_device(): lax.all_to_all(narrow_up, ROWS, split_axis=1, concat_axis=0, tiled=True)  5.32 us
  transfers between devices with their start and end apart: 1, of which 0 were waited for; matrix products, arithmetic and copies ran while one was open for 1% of the time, Pallas kernels for 0%

commit v1 on v0

--- a/solution.py
+++ b/solution.py
@@ -29,7 +29,10 @@
 def stacked_from(x, axes, sequence):
     pieces = x[None]
     for k in sequence:
-        pieces = lax.all_gather(pieces, axes[k], axis=0, tiled=True)
+        peers = lax.axis_size(axes[k])
+        blocks = jnp.stack([pieces for _ in range(peers)])
+        blocks = lax.all_to_all(blocks, axes[k], split_axis=0, concat_axis=0)
+        pieces = jnp.concatenate(blocks, axis=0)
     block = [lax.axis_size(axes[k]) for k in reversed(sequence)]
     pieces = pieces.reshape(*block, *x.shape)
     turned = sorted(range(len(sequence)), key=lambda place: sequence[len(sequence) - 1 - place])

time: 199 us -> 204 us (1.025)
  the two profiles are of different devices: /device:TPU:1 before, /device:TPU:11 now
where the time goes in v1:
time: 204 us; the launch traced here: 203 us
  waiting for transfers between devices  126 us (62%)
  starting transfers between devices  22.9 us (11%)
  blocking collectives  21.6 us (11%)
  local copies, waits for them, and re-layouts  15.8 us (8%)
  other arithmetic  8.68 us (4%)
  matrix products  8.04 us (4%)
    all_to_all x1, waiting for transfers between devices, per_device(): lax.all_to_all(narrow_up, ROWS, split_axis=1, concat_axis=0, tiled=True)  108 us
    all_to_all x2, blocking collectives, stacked_from(): blocks = lax.all_to_all(blocks, axes[k], split_axis=0, concat_axis=0)  21.6 us
    all_to_all x1, waiting for transfers between devices, copy_for_each(): return lax.all_to_all(copies, axis, split_axis=0, concat_axis=0, tiled=True)  17.4 us
    all_to_all x2, starting transfers between devices, stacked_from(): blocks = lax.all_to_all(blocks, axes[k], split_axis=0, concat_axis=0)  13.1 us
    dot_general x1, matrix products, per_device(): jnp.dot(low_up, high_up, preferred_element_type=jnp.float32)  8.04 us
    convert_element_type x1, other arithmetic, per_device(): narrow_up = (fresh_up / scale_up).astype(jnp.bfloat16)  6.83 us
    convert_element_type x1, local copies, waits for them, and re-layouts, per_device(): narrow_up = (fresh_up / scale_up).astype(jnp.bfloat16)  6.69 us
    all_to_all x1, local copies, waits for them, and re-layouts, per_device(): lax.all_to_all(narrow_up, ROWS, split_axis=1, concat_axis=0, tiled=True)  5.32 us
  transfers between devices with their start and end apart: 4, of which 2 were waited for; matrix products, arithmetic and copies ran while one was open for 12% of the time, Pallas kernels for 0%

profile of v1, /device:TPU:11, one launch (start us, length us, event | category | flops | bytes accessed | tf_op | source)
XLA Modules:
  0.0 203.4 jit_solution(12660332482941651942)
XLA Ops:
  0.6 0.0 copy-start
  0.6 0.7 add_convert_fusion
  1.4 7.1 %all_to_all.45 = bf16[4,1,48]{2,1,0:T(2,128)(2,1)S(1)} all-to-all(bf16[4,1,48]{2,1,0:T(2,128)(2,1)S(1)} %stack.12), channel_id=1, replica_groups=mesh['rows_0'=8,'rows_1'=4,'cols_0'=4,'cols_1'=2] {'rows_1'}, dimensions={0} | all-to-all | bytes 768 | tf_op jit(solution)/shard_map/all_to_all | solution.py:34
  8.5 14.6 %all_to_all.46 = bf16[8,4,48]{2,1,0:T(4,128)(2,1)S(1)} all-to-all(bf16[8,4,48]{2,1,0:T(4,128)(2,1)S(1)} %stack.13), channel_id=1, replica_groups=mesh['rows_0'=8,'rows_1'=4,'cols_0'=4,'cols_1'=2] {'rows_0'}, dimensions={0} | all-to-all | bytes 6144 | tf_op jit(solution)/shard_map/all_to_all | solution.py:34
  23.1 0.7 reshape.22
  23.8 4.3 %all-to-all-start.4 = ((bf16[4,2,768]{2,1,0:T(2,128)(2,1)}), bf16[4,2,768]{2,1,0:T(2,128)(2,1)S(1)}, u32[]{:S(2)}, u32[]{:S(2)}) async-start(bf16[4,2,768]{2,1,0:T(2,128)(2,1)} %reshape.22), calls=%async_computation.4 | async-start | bytes 24576 | tf_op jit(solution)/shard_map/all_to_all | solution.py:34
  28.0 0.0 copy-done
  28.0 8.0 %multiply_reduce_fusion = (f32[6144]{0:T(1024)S(1)}, f32[384,6144]{1,0:T(8,128)}) fusion(bf16[384,64]{0,1:T(8,128)(2,1)} %param.6, bf16[64,6144]{1,0:T(8,128)(2,1)S(1)} %copy-done, bf16[384,6144]{1,0:T(8,128)(2,1)} %param.5), kind=kOutput, calls=%fused_computation.1 | convolution fusion | flops 313780224 | bytes 15015936 | tf_op jit(solution)/shard_map/dot_general | solution.py:47
  36.1 0.0 all-to-all-done.4
  36.1 1.3 broadcast_in_dim.4
  37.4 4.7 %all-to-all-start = ((f32[32,1,6144]{2,1,0:T(1,128)}), f32[32,1,6144]{2,1,0:T(1,128)S(1)}, u32[]{:S(2)}, u32[]{:S(2)}) async-start(f32[32,1,6144]{2,1,0:T(1,128)} %broadcast_in_dim.4), calls=%async_computation | async-start | bytes 1572864 | tf_op jit(solution)/shard_map/all_to_all | solution.py:16
  42.1 0.1 reshape.23
  42.2 0.1 copy.33
  42.3 0.6 pad_maximum_fusion
  42.9 17.4 %all-to-all-done = f32[32,1,6144]{2,1,0:T(1,128)S(1)} async-done(((f32[32,1,6144]{2,1,0:T(1,128)}), f32[32,1,6144]{2,1,0:T(1,128)S(1)}, u32[]{:S(2)}, u32[]{:S(2)}) %all-to-all-start) | async-done | bytes 786464 | tf_op jit(solution)/shard_map/all_to_all | solution.py:16
  60.3 8.8 %all-to-all-start.5 = ((bf16[2,128,48]{1,2,0:T(8,128)(2,1)}), bf16[2,128,48]{1,2,0:T(8,128)(2,1)S(1)}, u32[]{:S(2)}, u32[]{:S(2)}) async-start(bf16[2,128,48]{1,2,0:T(8,128)(2,1)} %pad_maximum_fusion), calls=%async_computation.5 | async-start | bytes 49152 | tf_op jit(solution)/shard_map/all_to_all | solution.py:34
  69.1 0.5 reduce_sum.19
  69.6 6.8 %divide_convert_fusion = bf16[384,6144]{1,0:T(8,128)(2,1)} fusion(f32[384,6144]{1,0:T(8,128)} %get-tuple-element.4, f32[6144]{0:T(1024)S(1)} %sqrt.7), kind=kLoop, calls=%fused_computation | loop fusion | flops 4718592 | bytes 14180352 | tf_op jit(solution)/shard_map/convert_element_type | solution.py:52
  76.4 6.7 %copy.31 = bf16[384,6144]{0,1:T(8,128)(2,1)} copy(bf16[384,6144]{1,0:T(8,128)(2,1)} %divide_convert_fusion) | data formatting | bytes 9437184 | tf_op jit(solution)/shard_map/convert_element_type | solution.py:52
  83.1 0.0 all-to-all-done.5
  83.1 5.1 %all-to-all-start.1 = ((bf16[384,32,192]{0,2,1:T(8,128)(2,1)}), bf16[384,32,192]{0,2,1:T(8,128)(2,1)}, u32[]{:S(2)}, u32[]{:S(2)}) async-start(bf16[384,32,192]{0,2,1:T(8,128)(2,1)} %bitcast.14), calls=%async_computation.1 | async-start | bytes 9437184 | tf_op jit(solution)/shard_map/all_to_all | solution.py:53
  88.2 0.1 copy.35
  88.3 0.1 copy.36
  88.4 0.7 reshape_reshape.7
  89.1 0.6 dynamic_slice.3
  89.8 108.3 %all-to-all-done.1 = bf16[384,32,192]{0,2,1:T(8,128)(2,1)} async-done(((bf16[384,32,192]{0,2,1:T(8,128)(2,1)}), bf16[384,32,192]{0,2,1:T(8,128)(2,1)}, u32[]{:S(2)}, u32[]{:S(2)}) %all-to-all-start.1) | async-done | bytes 4718624 | tf_op jit(solution)/shard_map/all_to_all | solution.py:53
  198.0 5.3 %copy.39 = bf16[32,24,8,384]{3,2,0,1:T(8,128)(2,1)} copy(bf16[32,24,8,384]{3,2,1,0:T(8,128)(2,1)} %bitcast.8) | data formatting | bytes 9437184 | tf_op jit(solution)/shard_map/all_to_all | solution.py:53
  (5 shorter events, 0.0 us)
Async XLA Ops:
  0.6 27.4 %copy-start = (bf16[64,6144]{1,0:T(8,128)(2,1)S(1)}, bf16[64,6144]{1,0:T(8,128)(2,1)}, u32[]{:S(2)}) copy-start(bf16[64,6144]{1,0:T(8,128)(2,1)} %param.7) | copy-start | bytes 2359300
  23.8 12.3 %all-to-all-start.4 = ((bf16[4,2,768]{2,1,0:T(2,128)(2,1)}), bf16[4,2,768]{2,1,0:T(2,128)(2,1)S(1)}, u32[]{:S(2)}, u32[]{:S(2)}) async-start(bf16[4,2,768]{2,1,0:T(2,128)(2,1)} %reshape.22), calls=%async_computation.4 | async-start | bytes 24576 | tf_op jit(solution)/shard_map/all_to_all | solution.py:34
  37.4 22.9 %all-to-all-start = ((f32[32,1,6144]{2,1,0:T(1,128)}), f32[32,1,6144]{2,1,0:T(1,128)S(1)}, u32[]{:S(2)}, u32[]{:S(2)}) async-start(f32[32,1,6144]{2,1,0:T(1,128)} %broadcast_in_dim.4), calls=%async_computation | async-start | bytes 1572864 | tf_op jit(solution)/shard_map/all_to_all | solution.py:16
  60.3 22.8 %all-to-all-start.5 = ((bf16[2,128,48]{1,2,0:T(8,128)(2,1)}), bf16[2,128,48]{1,2,0:T(8,128)(2,1)S(1)}, u32[]{:S(2)}, u32[]{:S(2)}) async-start(bf16[2,128,48]{1,2,0:T(8,128)(2,1)} %pad_maximum_fusion), calls=%async_computation.5 | async-start | bytes 49152 | tf_op jit(solution)/shard_map/all_to_all | solution.py:34
  83.1 114.9 %all-to-all-start.1 = ((bf16[384,32,192]{0,2,1:T(8,128)(2,1)}), bf16[384,32,192]{0,2,1:T(8,128)(2,1)}, u32[]{:S(2)}, u32[]{:S(2)}) async-start(bf16[384,32,192]{0,2,1:T(8,128)(2,1)} %bitcast.14), calls=%async_computation.1 | async-start | bytes 9437184 | tf_op jit(solution)/shard_map/all_to_all | solution.py:53
